TPU v7x, 32 devices: a whole 2x2x4 slice. The times are simulated.
32 devices in a mesh: cp: 8 (over z, y), tp: 4 (over x, core).
Axes of the slice: x: 2, y: 2, z: 4, core: 2. Of those that a mesh axis runs over, the one named last changes fastest.
Arguments:
- query_rows: bfloat16 [4096, 16384], P(('cp', 'tp')), may hold values from -48 to 48
- token_keys: bfloat16 [4096, 1024], P(('cp', 'tp')), may hold values from -5 to 5
- token_values: bfloat16 [4096, 1024], P(('cp', 'tp')), may hold values from -5 to 5
- doc_lengths: int32 [4], replicated, may hold values from 1 to 2048, 4096 in all
- block_plan: int32 [8, 8], replicated, may hold values from 0 to 7, each once within a row
Outputs:
- attended: bfloat16 [4096, 16384], P(('cp', 'tp'))
Inputs may be any that keep to these rules, and one draw needn't show every extreme that they name: `doc_lengths`: the documents fill all 4096 tokens; one of them holds exactly 2048. Each row of block_plan is a permutation of 0 to 7.
All inputs are finite; a program needn't handle non-finite values.
Results may differ from a plain program's by a relative error of at most 0.012.
Values may be sent and summed in bfloat16 or wider, within the bound.
A program may use at most 128 MiB of HBM per device.

v0:
```python
import math

import jax
import jax.numpy as jnp
import numpy as np
from jax import lax
from jax.sharding import PartitionSpec as P

HEAD_SIZE = 128
DOC_MOST = 2048


def shifted(x, axis, by):
    peers = lax.axis_size(axis)
    pairs = [(i, i + by) for i in range(peers) if 0 <= i + by < peers]
    return lax.ppermute(x, axis, pairs)


def as_sent(x):

    def short(part):
        return part.astype(jnp.bfloat16) if part.dtype == jnp.float32 else part

    return jax.tree.map(short, x)


def scaled_frequencies(head_width):
    exponents = np.arange(0, head_width, 2) / head_width
    inverse = 1.0 / np.power(500000.0, exponents)
    wavelength = 2.0 * np.pi / inverse
    smooth = (8192.0 / wavelength - 1.0) / 3.0
    blended = (1.0 - smooth) * inverse / 8.0 + smooth * inverse
    middle = np.where(wavelength > 8192.0, inverse / 8.0, blended)
    return np.where(wavelength < 2048.0, inverse, middle)


def rotation_tables(head_width, length):
    frequencies = scaled_frequencies(head_width)
    coarse_count = (length + 127) // 128
    coarse_angle = np.arange(coarse_count)[:, None] * 128.0 * frequencies[None, :]
    fine_angle = np.arange(128)[:, None] * 1.0 * frequencies[None, :]
    return (np.cos(coarse_angle), np.sin(coarse_angle), np.cos(fine_angle), np.sin(fine_angle))


def rotation_rows(positions, head_width, length):
    tables = rotation_tables(head_width, length)
    coarse_count = tables[0].shape[0]
    upper_hit = (
        (positions // 128)[:, None] == jnp.arange(coarse_count, dtype=jnp.int32)[None, :]
    ).astype(jnp.float32)
    lower_hit = ((positions % 128)[:, None] == jnp.arange(128, dtype=jnp.int32)[None, :]).astype(
        jnp.float32
    )
    picked = []
    for lookup_table, selector in zip(tables, (upper_hit, upper_hit, lower_hit, lower_hit)):
        picked.append(
            jnp.dot(
                selector, jnp.asarray(lookup_table, jnp.float32), precision=lax.Precision.HIGHEST
            )
        )
    cosine_rows = picked[0] * picked[2] - picked[1] * picked[3]
    sine_table = picked[1] * picked[2] + picked[0] * picked[3]
    return (cosine_rows, sine_table)


def apply_rotary_heads(head_rows, cosine_rows, sine_table):
    half_width = head_rows.shape[-1] // 2
    first_half = head_rows[..., :half_width]
    second_half = head_rows[..., half_width:]
    cosine_rows = cosine_rows[:, None, :]
    sine_table = sine_table[:, None, :]
    return jnp.concatenate(
        [
            first_half * cosine_rows - second_half * sine_table,
            second_half * cosine_rows + first_half * sine_table,
        ],
        axis=-1,
    )


def attend(query_tile, query_pos, key_window, value_window, key_pos, doc_starts):
    first_pos = jnp.max(
        jnp.where(doc_starts[None, :] <= query_pos[:, None], doc_starts[None, :], 0), axis=1
    )
    scores = jnp.einsum(
        "rghd,wgd->ghrw", query_tile, key_window, preferred_element_type=jnp.float32
    ) * (1.0 / math.sqrt(HEAD_SIZE))
    allowed = (key_pos[None, :] <= query_pos[:, None]) & (key_pos[None, :] >= first_pos[:, None])
    masked = jnp.where(allowed, scores, -1e30)
    highest = jnp.max(masked, axis=3, keepdims=True)
    raised = jnp.where(allowed, jnp.exp(masked - highest), 0.0)
    totals = jnp.sum(raised, axis=3)
    weights = raised.astype(jnp.bfloat16)
    mixed_values = jnp.einsum(
        "ghrw,wgd->rghd", weights, value_window, preferred_element_type=jnp.float32
    )
    return (mixed_values / jnp.transpose(totals, (2, 0, 1))[..., None]).astype(jnp.bfloat16)


def on_device(query_rows, token_keys, token_values, doc_lengths, block_plan):
    query_heads, key_heads, value_heads = (
        lax.all_to_all(query_rows, "tp", split_axis=1, concat_axis=0, tiled=True),
        lax.all_to_all(token_keys, "tp", split_axis=1, concat_axis=0, tiled=True),
        lax.all_to_all(token_values, "tp", split_axis=1, concat_axis=0, tiled=True),
    )
    block_rows = query_heads.shape[0]
    cp_count = lax.axis_size("cp")
    cp_index = lax.axis_index("cp")
    sequence = block_rows * cp_count
    sub_rows = block_rows // cp_count
    group_count = key_heads.shape[1] // HEAD_SIZE
    query_count = query_heads.shape[1] // HEAD_SIZE
    per_group = query_count // group_count
    positions = cp_index * block_rows + jnp.arange(block_rows, dtype=jnp.int32)
    cosine_rows, sine_table = rotation_rows(positions, HEAD_SIZE, sequence)
    rotated_queries = apply_rotary_heads(
        query_heads.astype(jnp.float32).reshape(block_rows, query_count, HEAD_SIZE),
        cosine_rows,
        sine_table,
    ).astype(jnp.bfloat16)
    rotary_keys = apply_rotary_heads(
        key_heads.astype(jnp.float32).reshape(block_rows, group_count, HEAD_SIZE),
        cosine_rows,
        sine_table,
    ).astype(jnp.bfloat16)
    grouped_values = value_heads.reshape(block_rows, group_count, HEAD_SIZE)
    doc_starts = jnp.cumsum(doc_lengths) - doc_lengths
    grouped_queries = rotated_queries.reshape(block_rows, group_count, per_group, HEAD_SIZE)
    plan_row = lax.dynamic_slice(block_plan, (cp_index, 0), (1, cp_count))[0]
    reach_blocks = DOC_MOST // block_rows
    earlier_keys = []
    earlier_values = []
    for distance in range(reach_blocks, 0, -1):
        moved_keys, moved_values = shifted((rotary_keys, grouped_values), "cp", distance)
        earlier_keys.append(moved_keys)
        earlier_values.append(moved_values)
    window_keys = jnp.concatenate(earlier_keys + [rotary_keys], axis=0)
    window_values = jnp.concatenate(earlier_values + [grouped_values], axis=0)
    window_pos = (cp_index - reach_blocks) * block_rows + jnp.arange(
        (reach_blocks + 1) * block_rows, dtype=jnp.int32
    )
    tile_rows = min(64, block_rows)
    window_span = DOC_MOST + tile_rows

    def attend_tile(tile_index):
        offset = tile_index * tile_rows
        return attend(
            lax.dynamic_slice_in_dim(grouped_queries, offset, tile_rows, 0),
            lax.dynamic_slice_in_dim(positions, offset, tile_rows, 0),
            lax.dynamic_slice_in_dim(window_keys, offset, window_span, 0),
            lax.dynamic_slice_in_dim(window_values, offset, window_span, 0),
            lax.dynamic_slice_in_dim(window_pos, offset, window_span, 0),
            doc_starts,
        )

    local_out = lax.map(attend_tile, jnp.arange(block_rows // tile_rows, dtype=jnp.int32))
    local_out = local_out.reshape(cp_count, sub_rows, query_count * HEAD_SIZE)
    outgoing = local_out[plan_row].reshape(block_rows, query_count * HEAD_SIZE)
    placed = lax.all_to_all(
        as_sent(outgoing), "cp", split_axis=0, concat_axis=0, tiled=True
    ).astype(outgoing.dtype)
    return lax.all_to_all(as_sent(placed), "tp", split_axis=0, concat_axis=1, tiled=True).astype(
        placed.dtype
    )


def solution(mesh):
    placed = (P(("cp", "tp"), None), P(("cp", "tp"), None), P(("cp", "tp"), None), P(), P())
    return jax.shard_map(
        on_device, mesh=mesh, in_specs=placed, out_specs=P(("cp", "tp"), None), check_vma=False
    )
```

profile of v0, /device:TPU:2, one launch (start us, length us, event | category | flops | bytes accessed | tf_op | source)
XLA Modules:
  0.0 485.7 jit_solution(6880734344970028301)
XLA Ops:
  18.7 6.6 %all-to-all-start.2 = ((bf16[128,4,4096]{2,0,1:T(8,128)(2,1)}), bf16[128,4,4096]{2,0,1:T(8,128)(2,1)}, u32[]{:S(2)}, u32[]{:S(2)}) async-start(bf16[128,4,4096]{2,0,1:T(8,128)(2,1)} %bitcast.100), calls=%async_computation.2 | async-start | bytes 8388608 | tf_op jit(solution)/shard_map/all_to_all | solution.py:102
  45.7 10.5 %collective-permute-start.1 = (bf16[512,2,128]{2,1,0:T(2,128)(2,1)S(1)}, bf16[512,2,128]{2,1,0:T(2,128)(2,1)S(1)}, u32[]{:S(2)}, u32[]{:S(2)}) collective-permute-start(bf16[512,2,128]{2,1,0:T(2,128)(2,1)S(1)} %reshape.133), channel_id=1, source_target_pairs={{0,12},{4,16},{8,20},{12,24},{16,28},{1,13},{5,17},{9,21},{13,25},... | collective-permute-start | bytes 786440 | tf_op jit(solution)/shard_map/ppermute | solution.py:16
  87.6 192.5 %while.10 = (s32[]{:T(128)}, bf16[8,64,2,16,128]{4,3,2,1,0:T(8,128)(2,1)}, s32[8]{0:T(128)S(1)}, bf16[2560,2,128]{2,1,0:T(2,128)(2,1)}, s32[2560]{0:T(1024)S(1)}...) while((s32[]{:T(128)}, ...), condition=%wide.region_5.6_spmd, body=%wide.region_1.5_spmd.sunk | while | flops 2241477376 | bytes 26344440 | solution.py:156
  93.0 11.5 %fusion.60 = (f32[2,16,64]{2,1,0:T(8,128)S(1)}, bf16[2,16,64,2112]{3,2,1,0:T(8,128)(2,1)}) fusion(pred[64,2112]{1,0:T(8,128)(4,1)} %compare_and_fusion.2, bf16[2112,2,128]{2,1,0:T(2,128)(2,1)S(1)} %get-tuple-element.171, bf16[512,2,16,128]{3,0,2,1:T(8,128)(2,1)} %get-tuple-element.211, s32[]{:T(128)S(6)} %select_n.81), kind=kOutput, calls=%fused_computation.76.clone.1 | convolution fusion | flops 1133250560 | bytes 10543108 | tf_op jit(solution)/shard_map/while/body/eval_jaxpr/sub | solution.py:91
  104.5 6.0 %fusion.61 = bf16[1,64,2,16,128]{4,1,3,2,0:T(8,128)(2,1)S(1)} fusion(bf16[2,16,64,2112]{3,2,1,0:T(8,128)(2,1)} %get-tuple-element.172, bf16[2112,2,128]{2,1,0:T(2,128)(2,1)S(1)} %get-tuple-element.173, f32[64,2,16]{0,2,1:T(8,128)S(1)} %bitcast.109), kind=kOutput, calls=%fused_computation.14.clone.1 | convolution fusion | flops 1107820544 | bytes 10264576 | tf_op jit(solution)/shard_map/while/body/eval_jaxpr/ghrw,wgd->rghd/dot_general | solution.py:94
  117.1 11.5 %fusion.60 = (f32[2,16,64]{2,1,0:T(8,128)S(1)}, bf16[2,16,64,2112]{3,2,1,0:T(8,128)(2,1)}) fusion(pred[64,2112]{1,0:T(8,128)(4,1)} %compare_and_fusion.2, bf16[2112,2,128]{2,1,0:T(2,128)(2,1)S(1)} %get-tuple-element.171, bf16[512,2,16,128]{3,0,2,1:T(8,128)(2,1)} %get-tuple-element.211, s32[]{:T(128)S(6)} %select_n.81), kind=kOutput, calls=%fused_computation.76.clone.1 | convolution fusion | flops 1133250560 | bytes 10543108 | tf_op jit(solution)/shard_map/while/body/eval_jaxpr/sub | solution.py:91
  128.6 6.0 %fusion.61 = bf16[1,64,2,16,128]{4,1,3,2,0:T(8,128)(2,1)S(1)} fusion(bf16[2,16,64,2112]{3,2,1,0:T(8,128)(2,1)} %get-tuple-element.172, bf16[2112,2,128]{2,1,0:T(2,128)(2,1)S(1)} %get-tuple-element.173, f32[64,2,16]{0,2,1:T(8,128)S(1)} %bitcast.109), kind=kOutput, calls=%fused_computation.14.clone.1 | convolution fusion | flops 1107820544 | bytes 10264576 | tf_op jit(solution)/shard_map/while/body/eval_jaxpr/ghrw,wgd->rghd/dot_general | solution.py:94
  141.2 11.5 %fusion.60 = (f32[2,16,64]{2,1,0:T(8,128)S(1)}, bf16[2,16,64,2112]{3,2,1,0:T(8,128)(2,1)}) fusion(pred[64,2112]{1,0:T(8,128)(4,1)} %compare_and_fusion.2, bf16[2112,2,128]{2,1,0:T(2,128)(2,1)S(1)} %get-tuple-element.171, bf16[512,2,16,128]{3,0,2,1:T(8,128)(2,1)} %get-tuple-element.211, s32[]{:T(128)S(6)} %select_n.81), kind=kOutput, calls=%fused_computation.76.clone.1 | convolution fusion | flops 1133250560 | bytes 10543108 | tf_op jit(solution)/shard_map/while/body/eval_jaxpr/sub | solution.py:91
  152.7 6.0 %fusion.61 = bf16[1,64,2,16,128]{4,1,3,2,0:T(8,128)(2,1)S(1)} fusion(bf16[2,16,64,2112]{3,2,1,0:T(8,128)(2,1)} %get-tuple-element.172, bf16[2112,2,128]{2,1,0:T(2,128)(2,1)S(1)} %get-tuple-element.173, f32[64,2,16]{0,2,1:T(8,128)S(1)} %bitcast.109), kind=kOutput, calls=%fused_computation.14.clone.1 | convolution fusion | flops 1107820544 | bytes 10264576 | tf_op jit(solution)/shard_map/while/body/eval_jaxpr/ghrw,wgd->rghd/dot_general | solution.py:94
  165.2 11.5 %fusion.60 = (f32[2,16,64]{2,1,0:T(8,128)S(1)}, bf16[2,16,64,2112]{3,2,1,0:T(8,128)(2,1)}) fusion(pred[64,2112]{1,0:T(8,128)(4,1)} %compare_and_fusion.2, bf16[2112,2,128]{2,1,0:T(2,128)(2,1)S(1)} %get-tuple-element.171, bf16[512,2,16,128]{3,0,2,1:T(8,128)(2,1)} %get-tuple-element.211, s32[]{:T(128)S(6)} %select_n.81), kind=kOutput, calls=%fused_computation.76.clone.1 | convolution fusion | flops 1133250560 | bytes 10543108 | tf_op jit(solution)/shard_map/while/body/eval_jaxpr/sub | solution.py:91
  176.7 6.0 %fusion.61 = bf16[1,64,2,16,128]{4,1,3,2,0:T(8,128)(2,1)S(1)} fusion(bf16[2,16,64,2112]{3,2,1,0:T(8,128)(2,1)} %get-tuple-element.172, bf16[2112,2,128]{2,1,0:T(2,128)(2,1)S(1)} %get-tuple-element.173, f32[64,2,16]{0,2,1:T(8,128)S(1)} %bitcast.109), kind=kOutput, calls=%fused_computation.14.clone.1 | convolution fusion | flops 1107820544 | bytes 10264576 | tf_op jit(solution)/shard_map/while/body/eval_jaxpr/ghrw,wgd->rghd/dot_general | solution.py:94
  189.3 11.5 %fusion.60 = (f32[2,16,64]{2,1,0:T(8,128)S(1)}, bf16[2,16,64,2112]{3,2,1,0:T(8,128)(2,1)}) fusion(pred[64,2112]{1,0:T(8,128)(4,1)} %compare_and_fusion.2, bf16[2112,2,128]{2,1,0:T(2,128)(2,1)S(1)} %get-tuple-element.171, bf16[512,2,16,128]{3,0,2,1:T(8,128)(2,1)} %get-tuple-element.211, s32[]{:T(128)S(6)} %select_n.81), kind=kOutput, calls=%fused_computation.76.clone.1 | convolution fusion | flops 1133250560 | bytes 10543108 | tf_op jit(solution)/shard_map/while/body/eval_jaxpr/sub | solution.py:91
  200.8 6.0 %fusion.61 = bf16[1,64,2,16,128]{4,1,3,2,0:T(8,128)(2,1)S(1)} fusion(bf16[2,16,64,2112]{3,2,1,0:T(8,128)(2,1)} %get-tuple-element.172, bf16[2112,2,128]{2,1,0:T(2,128)(2,1)S(1)} %get-tuple-element.173, f32[64,2,16]{0,2,1:T(8,128)S(1)} %bitcast.109), kind=kOutput, calls=%fused_computation.14.clone.1 | convolution fusion | flops 1107820544 | bytes 10264576 | tf_op jit(solution)/shard_map/while/body/eval_jaxpr/ghrw,wgd->rghd/dot_general | solution.py:94
  213.3 11.5 %fusion.60 = (f32[2,16,64]{2,1,0:T(8,128)S(1)}, bf16[2,16,64,2112]{3,2,1,0:T(8,128)(2,1)}) fusion(pred[64,2112]{1,0:T(8,128)(4,1)} %compare_and_fusion.2, bf16[2112,2,128]{2,1,0:T(2,128)(2,1)S(1)} %get-tuple-element.171, bf16[512,2,16,128]{3,0,2,1:T(8,128)(2,1)} %get-tuple-element.211, s32[]{:T(128)S(6)} %select_n.81), kind=kOutput, calls=%fused_computation.76.clone.1 | convolution fusion | flops 1133250560 | bytes 10543108 | tf_op jit(solution)/shard_map/while/body/eval_jaxpr/sub | solution.py:91
  224.8 6.0 %fusion.61 = bf16[1,64,2,16,128]{4,1,3,2,0:T(8,128)(2,1)S(1)} fusion(bf16[2,16,64,2112]{3,2,1,0:T(8,128)(2,1)} %get-tuple-element.172, bf16[2112,2,128]{2,1,0:T(2,128)(2,1)S(1)} %get-tuple-element.173, f32[64,2,16]{0,2,1:T(8,128)S(1)} %bitcast.109), kind=kOutput, calls=%fused_computation.14.clone.1 | convolution fusion | flops 1107820544 | bytes 10264576 | tf_op jit(solution)/shard_map/while/body/eval_jaxpr/ghrw,wgd->rghd/dot_general | solution.py:94
  237.4 11.5 %fusion.60 = (f32[2,16,64]{2,1,0:T(8,128)S(1)}, bf16[2,16,64,2112]{3,2,1,0:T(8,128)(2,1)}) fusion(pred[64,2112]{1,0:T(8,128)(4,1)} %compare_and_fusion.2, bf16[2112,2,128]{2,1,0:T(2,128)(2,1)S(1)} %get-tuple-element.171, bf16[512,2,16,128]{3,0,2,1:T(8,128)(2,1)} %get-tuple-element.211, s32[]{:T(128)S(6)} %select_n.81), kind=kOutput, calls=%fused_computation.76.clone.1 | convolution fusion | flops 1133250560 | bytes 10543108 | tf_op jit(solution)/shard_map/while/body/eval_jaxpr/sub | solution.py:91
  248.9 6.0 %fusion.61 = bf16[1,64,2,16,128]{4,1,3,2,0:T(8,128)(2,1)S(1)} fusion(bf16[2,16,64,2112]{3,2,1,0:T(8,128)(2,1)} %get-tuple-element.172, bf16[2112,2,128]{2,1,0:T(2,128)(2,1)S(1)} %get-tuple-element.173, f32[64,2,16]{0,2,1:T(8,128)S(1)} %bitcast.109), kind=kOutput, calls=%fused_computation.14.clone.1 | convolution fusion | flops 1107820544 | bytes 10264576 | tf_op jit(solution)/shard_map/while/body/eval_jaxpr/ghrw,wgd->rghd/dot_general | solution.py:94
  261.5 11.5 %fusion.60 = (f32[2,16,64]{2,1,0:T(8,128)S(1)}, bf16[2,16,64,2112]{3,2,1,0:T(8,128)(2,1)}) fusion(pred[64,2112]{1,0:T(8,128)(4,1)} %compare_and_fusion.2, bf16[2112,2,128]{2,1,0:T(2,128)(2,1)S(1)} %get-tuple-element.171, bf16[512,2,16,128]{3,0,2,1:T(8,128)(2,1)} %get-tuple-element.211, s32[]{:T(128)S(6)} %select_n.81), kind=kOutput, calls=%fused_computation.76.clone.1 | convolution fusion | flops 1133250560 | bytes 10543108 | tf_op jit(solution)/shard_map/while/body/eval_jaxpr/sub | solution.py:91
  273.0 6.0 %fusion.61 = bf16[1,64,2,16,128]{4,1,3,2,0:T(8,128)(2,1)S(1)} fusion(bf16[2,16,64,2112]{3,2,1,0:T(8,128)(2,1)} %get-tuple-element.172, bf16[2112,2,128]{2,1,0:T(2,128)(2,1)S(1)} %get-tuple-element.173, f32[64,2,16]{0,2,1:T(8,128)S(1)} %bitcast.109), kind=kOutput, calls=%fused_computation.14.clone.1 | convolution fusion | flops 1107820544 | bytes 10264576 | tf_op jit(solution)/shard_map/while/body/eval_jaxpr/ghrw,wgd->rghd/dot_general | solution.py:94
  280.1 7.3 %reshape.136 = bf16[8,64,4096]{2,1,0:T(8,128)(2,1)} reshape(bf16[8,64,2,16,128]{4,3,2,1,0:T(8,128)(2,1)} %get-tuple-element.52) | data formatting | bytes 8388608 | tf_op jit(solution)/shard_map/reshape | solution.py:157
  292.4 130.2 %all_to_all.67 = bf16[8,64,4096]{2,1,0:T(8,128)(2,1)S(1)} all-to-all(bf16[8,64,4096]{2,1,0:T(8,128)(2,1)} %gather_fusion), channel_id=1, replica_groups=mesh['cp'=8,'tp'=4] {'cp'}, dimensions={0} | all-to-all | bytes 8388608 | tf_op jit(solution)/shard_map/all_to_all | solution.py:159
  422.6 50.3 %all_to_all.68 = bf16[4,128,4096]{2,1,0:T(8,128)(2,1)} all-to-all(bf16[4,128,4096]{2,1,0:T(8,128)(2,1)S(1)} %bitcast.101), channel_id=1, replica_groups=mesh['cp'=8,'tp'=4] {'tp'}, dimensions={0} | all-to-all | bytes 8388608 | tf_op jit(solution)/shard_map/all_to_all | solution.py:162
  472.9 6.4 %copy.52 = bf16[128,4,4096]{0,2,1:T(8,128)(2,1)} copy(bf16[128,4,4096]{2,0,1:T(8,128)(2,1)} %bitcast.102) | data formatting | bytes 8388608 | tf_op jit(solution)/shard_map/all_to_all | solution.py:162
  479.3 6.4 %copy.53 = bf16[128,16384]{1,0:T(8,128)(2,1)} copy(bf16[128,16384]{0,1:T(8,128)(2,1)} %bitcast.103) | data formatting | bytes 8388608 | tf_op jit(solution)/shard_map/all_to_all | solution.py:162
  (130 shorter events, 122.1 us)
Async XLA Ops:
  1.7 8.9 %all-to-all-start.1 = ((bf16[128,4,256]{2,0,1:T(8,128)(2,1)}), bf16[128,4,256]{2,0,1:T(8,128)(2,1)S(1)}, u32[]{:S(2)}, u32[]{:S(2)}) async-start(bf16[128,4,256]{2,0,1:T(8,128)(2,1)} %bitcast.78), calls=%async_computation.1 | async-start | bytes 524288 | tf_op jit(solution)/shard_map/all_to_all | solution.py:103
  5.1 4.7 copy-start
  5.1 9.3 %copy-start.3 = (f32[128,64]{1,0:T(8,128)S(1)}, f32[128,64]{1,0:T(8,128)}, u32[]{:S(2)}) copy-start(f32[128,64]{1,0:T(8,128)} %constant.85.clone) | copy-start | bytes 98308
  10.5 8.2 %all-to-all-start = ((bf16[128,4,256]{2,0,1:T(8,128)(2,1)}), bf16[128,4,256]{2,0,1:T(8,128)(2,1)S(1)}, u32[]{:S(2)}, u32[]{:S(2)}) async-start(bf16[128,4,256]{2,0,1:T(8,128)(2,1)} %bitcast.79), calls=%async_computation | async-start | bytes 524288 | tf_op jit(solution)/shard_map/all_to_all | solution.py:104
  18.7 6.6 %copy-start.4 = (f32[32,64]{1,0:T(8,128)S(1)}, f32[32,64]{1,0:T(8,128)}, u32[]{:S(2)}) copy-start(f32[32,64]{1,0:T(8,128)} %constant.82.clone) | copy-start | bytes 24580
  18.7 7.0 %copy-start.2 = (f32[128,64]{1,0:T(8,128)S(1)}, f32[128,64]{1,0:T(8,128)}, u32[]{:S(2)}) copy-start(f32[128,64]{1,0:T(8,128)} %constant.84.clone) | copy-start | bytes 98308
  18.7 7.4 %copy-start.5 = (f32[32,64]{1,0:T(8,128)S(1)}, f32[32,64]{1,0:T(8,128)}, u32[]{:S(2)}) copy-start(f32[32,64]{1,0:T(8,128)} %constant.83.clone) | copy-start | bytes 24580
  18.7 8.0 %copy-start.6 = (s32[4]{0:T(128)S(1)}, s32[4]{0:T(128)}, u32[]{:S(2)}) copy-start(s32[4]{0:T(128)} %param.14) | copy-start | bytes 52
  18.7 53.4 %all-to-all-start.2 = ((bf16[128,4,4096]{2,0,1:T(8,128)(2,1)}), bf16[128,4,4096]{2,0,1:T(8,128)(2,1)}, u32[]{:S(2)}, u32[]{:S(2)}) async-start(bf16[128,4,4096]{2,0,1:T(8,128)(2,1)} %bitcast.100), calls=%async_computation.2 | async-start | bytes 8388608 | tf_op jit(solution)/shard_map/all_to_all | solution.py:102
  28.8 16.1 %collective-permute-start.4 = (bf16[512,2,128]{2,1,0:T(2,128)(2,1)S(1)}, bf16[512,2,128]{2,1,0:T(2,128)(2,1)S(1)}, u32[]{:S(2)}, u32[]{:S(2)}) collective-permute-start(bf16[512,2,128]{2,1,0:T(2,128)(2,1)S(1)} %pad_maximum_fusion.1), channel_id=1, source_target_pairs={{0,16},{4,20},{8,24},{12,28},{1,17},{5,21},{9,25},{13,29},{2,18},{... | collective-permute-start | bytes 786440 | tf_op jit(solution)/shard_map/ppermute | solution.py:16
  34.6 22.7 %collective-permute-start.5 = (bf16[512,2,128]{2,1,0:T(2,128)(2,1)S(1)}, bf16[512,2,128]{2,1,0:T(2,128)(2,1)}, u32[]{:S(2)}, u32[]{:S(2)}) collective-permute-start(bf16[512,2,128]{2,1,0:T(2,128)(2,1)S(1)} %pad_maximum_fusion.1), channel_id=1, source_target_pairs={{0,12},{4,16},{8,20},{12,24},{16,28},{1,13},{5,17},{9,21},{13,25},... | collective-permute-start | bytes 786440 | tf_op jit(solution)/shard_map/ppermute | solution.py:16
  39.8 20.0 %collective-permute-start.6 = (bf16[512,2,128]{2,1,0:T(2,128)(2,1)S(1)}, bf16[512,2,128]{2,1,0:T(2,128)(2,1)S(1)}, u32[]{:S(2)}, u32[]{:S(2)}) collective-permute-start(bf16[512,2,128]{2,1,0:T(2,128)(2,1)S(1)} %pad_maximum_fusion.1), channel_id=1, source_target_pairs={{0,8},{4,12},{8,16},{12,20},{16,24},{20,28},{1,9},{5,13},{9,17},{1... | collective-permute-start | bytes 786440 | tf_op jit(solution)/shard_map/ppermute | solution.py:16
  41.1 24.6 %collective-permute-start.7 = (bf16[512,2,128]{2,1,0:T(2,128)(2,1)S(1)}, bf16[512,2,128]{2,1,0:T(2,128)(2,1)S(1)}, u32[]{:S(2)}, u32[]{:S(2)}) collective-permute-start(bf16[512,2,128]{2,1,0:T(2,128)(2,1)S(1)} %pad_maximum_fusion.1), channel_id=1, source_target_pairs={{0,4},{4,8},{8,12},{12,16},{16,20},{20,24},{24,28},{1,5},{5,9},{9,... | collective-permute-start | bytes 786440 | tf_op jit(solution)/shard_map/ppermute | solution.py:16
  43.6 22.6 %collective-permute-start = (bf16[512,2,128]{2,1,0:T(2,128)(2,1)S(1)}, bf16[512,2,128]{2,1,0:T(2,128)(2,1)S(1)}, u32[]{:S(2)}, u32[]{:S(2)}) collective-permute-start(bf16[512,2,128]{2,1,0:T(2,128)(2,1)S(1)} %reshape.133), channel_id=1, source_target_pairs={{0,16},{4,20},{8,24},{12,28},{1,17},{5,21},{9,25},{13,29},{2,18},{... | collective-permute-start | bytes 786440 | tf_op jit(solution)/shard_map/ppermute | solution.py:16
  44.9 0.7 copy-start.1
  45.7 21.4 %collective-permute-start.1 = (bf16[512,2,128]{2,1,0:T(2,128)(2,1)S(1)}, bf16[512,2,128]{2,1,0:T(2,128)(2,1)S(1)}, u32[]{:S(2)}, u32[]{:S(2)}) collective-permute-start(bf16[512,2,128]{2,1,0:T(2,128)(2,1)S(1)} %reshape.133), channel_id=1, source_target_pairs={{0,12},{4,16},{8,20},{12,24},{16,28},{1,13},{5,17},{9,21},{13,25},... | collective-permute-start | bytes 786440 | tf_op jit(solution)/shard_map/ppermute | solution.py:16
  57.3 10.7 %collective-permute-start.2 = (bf16[512,2,128]{2,1,0:T(2,128)(2,1)S(1)}, bf16[512,2,128]{2,1,0:T(2,128)(2,1)S(1)}, u32[]{:S(2)}, u32[]{:S(2)}) collective-permute-start(bf16[512,2,128]{2,1,0:T(2,128)(2,1)S(1)} %reshape.133), channel_id=1, source_target_pairs={{0,8},{4,12},{8,16},{12,20},{16,24},{20,28},{1,9},{5,13},{9,17},{1... | collective-permute-start | bytes 786440 | tf_op jit(solution)/shard_map/ppermute | solution.py:16
  59.8 10.6 %collective-permute-start.3 = (bf16[512,2,128]{2,1,0:T(2,128)(2,1)S(1)}, bf16[512,2,128]{2,1,0:T(2,128)(2,1)S(1)}, u32[]{:S(2)}, u32[]{:S(2)}) collective-permute-start(bf16[512,2,128]{2,1,0:T(2,128)(2,1)S(1)} %reshape.133), channel_id=1, source_target_pairs={{0,4},{4,8},{8,12},{12,16},{16,20},{20,24},{24,28},{1,5},{5,9},{9,... | collective-permute-start | bytes 786440 | tf_op jit(solution)/shard_map/ppermute | solution.py:16
where the time goes:
time: 491 us; the launch traced here: 486 us
  blocking collectives  181 us (37%)
  matrix products  141 us (29%)
  local copies, waits for them, and re-layouts  85.5 us (17%)
  starting transfers between devices  46.6 us (9%)
  other arithmetic  20.1 us (4%)
  loops' own time  5.85 us (1%)
  waiting for transfers between devices  5.54 us (1%)
    all_to_all x1, blocking collectives, on_device(): lax.all_to_all(as_sent(outgoing), 'cp', split_axis=0, concat_axis=0, tile...  130 us
    sub x8, matrix products, attend(): raised = jnp.where(allowed, jnp.exp(masked - highest), 0.0)  92 us
    all_to_all x1, blocking collectives, on_device(): lax.all_to_all(as_sent(placed), 'tp', split_axis=0, concat_axis=1, tiled=...  50.3 us
    dot_general x8, matrix products, attend(): jnp.einsum('ghrw,wgd->rghd', weights, value_window, preferred_element_typ...  47.7 us
    ppermute x8, starting transfers between devices, shifted(): return lax.ppermute(x, axis, pairs)  32.8 us
    dynamic_slice x8, local copies, waits for them, and re-layouts, attend_tile(): lax.dynamic_slice_in_dim(window_keys, offset, window_span, 0)  23.8 us
    all_to_all x2, local copies, waits for them, and re-layouts, on_device(): lax.all_to_all(as_sent(placed), 'tp', split_axis=0, concat_axis=1, tiled=...  12.7 us
  transfers between devices with their start and end apart: 11, of which 2 were waited for; matrix products, arithmetic and copies ran while one was open for 4% of the time, Pallas kernels for 0%

commit v1 on v0

v1 whole, which is shorter than its diff:
```python
import functools
import math

import jax
import jax.numpy as jnp
import numpy as np
from jax import lax
from jax.experimental import pallas as pl
from jax.experimental.pallas import tpu as pltpu
from jax.sharding import PartitionSpec as P

HEAD_SIZE = 128
DOC_MOST = 2048


def shifted(x, axis, by):
    peers = lax.axis_size(axis)
    pairs = [(i, i + by) for i in range(peers) if 0 <= i + by < peers]
    return lax.ppermute(x, axis, pairs)


def scaled_frequencies(head_width):
    exponents = np.arange(0, head_width, 2) / head_width
    inverse = 1.0 / np.power(500000.0, exponents)
    wavelength = 2.0 * np.pi / inverse
    smooth = (8192.0 / wavelength - 1.0) / 3.0
    blended = (1.0 - smooth) * inverse / 8.0 + smooth * inverse
    middle = np.where(wavelength > 8192.0, inverse / 8.0, blended)
    return np.where(wavelength < 2048.0, inverse, middle)


def rotation_tables(head_width, length):
    frequencies = scaled_frequencies(head_width)
    coarse_count = (length + 127) // 128
    coarse_angle = np.arange(coarse_count)[:, None] * 128.0 * frequencies[None, :]
    fine_angle = np.arange(128)[:, None] * 1.0 * frequencies[None, :]
    return (np.cos(coarse_angle), np.sin(coarse_angle), np.cos(fine_angle), np.sin(fine_angle))


def rotation_rows(positions, head_width, length):
    tables = rotation_tables(head_width, length)
    coarse_count = tables[0].shape[0]
    upper_hit = (
        (positions // 128)[:, None] == jnp.arange(coarse_count, dtype=jnp.int32)[None, :]
    ).astype(jnp.float32)
    lower_hit = ((positions % 128)[:, None] == jnp.arange(128, dtype=jnp.int32)[None, :]).astype(
        jnp.float32
    )
    picked = []
    for lookup_table, selector in zip(tables, (upper_hit, upper_hit, lower_hit, lower_hit)):
        picked.append(
            jnp.dot(
                selector, jnp.asarray(lookup_table, jnp.float32), precision=lax.Precision.HIGHEST
            )
        )
    cosine_rows = picked[0] * picked[2] - picked[1] * picked[3]
    sine_table = picked[1] * picked[2] + picked[0] * picked[3]
    return (cosine_rows, sine_table)


def apply_rotary_heads(head_rows, cosine_rows, sine_table):
    half_width = head_rows.shape[-1] // 2
    first_half = head_rows[..., :half_width]
    second_half = head_rows[..., half_width:]
    cosine_rows = cosine_rows[:, None, :]
    sine_table = sine_table[:, None, :]
    return jnp.concatenate(
        [
            first_half * cosine_rows - second_half * sine_table,
            second_half * cosine_rows + first_half * sine_table,
        ],
        axis=-1,
    )


def attend_and_place(cp_count, tp_count, shape, plan_ref, query_ref, cosine_ref, sine_ref, mark_ref,
                     key_ref, value_ref, out_ref, outbox, send_sem, recv_sem, own_sem):
    block_rows, sub_rows, groups, per_group, window = shape
    cp_index = lax.axis_index("cp")
    tp_index = lax.axis_index("tp")
    held = cp_count // tp_count
    width = per_group * HEAD_SIZE
    target_tp = cp_index // held
    sub_here = cp_index % held
    steps = cp_count * groups
    batch = max(1, min(per_group, 512 // sub_rows))
    tile = batch * sub_rows
    past = window - sub_rows

    def target_of(order):
        if cp_count % 2:
            return lax.rem(cp_index + order, cp_count)
        half = cp_count // 2
        side = lax.rem(cp_index // half + 1 + order // half, 2)
        return side * half + lax.rem(cp_index + order, half)

    def remote(step, target_cp):
        group = lax.rem(step, groups)
        column = pl.multiple_of((tp_index * groups + group) * width, width)
        row = pl.multiple_of(sub_here * sub_rows, sub_rows)
        slot = (sub_here * tp_count + tp_index) * groups + group
        return pltpu.make_async_remote_copy(
            src_ref=outbox.at[step],
            dst_ref=out_ref.at[pl.ds(row, sub_rows), pl.ds(column, width)],
            send_sem=send_sem.at[step],
            recv_sem=recv_sem.at[slot],
            device_id=(target_cp, target_tp),
            device_id_type=pl.DeviceIdType.MESH,
        )

    def local(step):
        group = lax.rem(step, groups)
        column = pl.multiple_of((tp_index * groups + group) * width, width)
        row = pl.multiple_of(sub_here * sub_rows, sub_rows)
        return pltpu.make_async_copy(
            outbox.at[step],
            out_ref.at[pl.ds(row, sub_rows), pl.ds(column, width)],
            own_sem.at[group],
        )

    def is_self(target_cp):
        return jnp.logical_and(target_cp == cp_index, target_tp == tp_index)

    def one_step(step, carry):
        order = step // groups
        group = lax.rem(step, groups)
        target_cp = target_of(order)
        piece = plan_ref[cp_index, target_cp]
        cosine = cosine_ref[piece]
        sine = sine_ref[piece]
        mark = mark_ref[piece]
        reach = window // sub_rows
        keys = key_ref[group, pl.ds(piece, reach)].reshape(window, 2 * HEAD_SIZE)
        values = value_ref[group, pl.ds(piece, reach)].reshape(window, HEAD_SIZE)
        causal = lax.broadcasted_iota(jnp.int32, (sub_rows, sub_rows), 1) <= lax.broadcasted_iota(
            jnp.int32, (sub_rows, sub_rows), 0
        )
        causal_all = jnp.concatenate([causal.astype(jnp.float32)] * batch, axis=0) > 0.5
        for part in range(per_group // batch):
            rotated = []
            for head in range(batch):
                column = pl.multiple_of(group * width, width) + (part * batch + head) * HEAD_SIZE
                column = pl.multiple_of(column, HEAD_SIZE)
                raw = query_ref[piece, :, pl.ds(column, HEAD_SIZE)].astype(jnp.float32)
                turned = raw * cosine + pltpu.roll(raw, HEAD_SIZE // 2, 1) * sine
                rotated.append(jnp.concatenate([turned.astype(jnp.bfloat16), mark], axis=1))
            queries = jnp.concatenate(rotated, axis=0)
            nt = (((1,), (1,)), ((), ()))
            early = lax.dot_general(queries, keys[:past], nt, preferred_element_type=jnp.float32)
            late = lax.dot_general(queries, keys[past:], nt, preferred_element_type=jnp.float32)
            late = jnp.where(causal_all, late, -1e30)
            highest = jnp.maximum(
                jnp.max(early, axis=1, keepdims=True), jnp.max(late, axis=1, keepdims=True)
            )
            early = jnp.exp2(early - highest)
            late = jnp.exp2(late - highest)
            totals = jnp.sum(early, axis=1, keepdims=True) + jnp.sum(late, axis=1, keepdims=True)
            mixed = jnp.dot(early.astype(jnp.bfloat16), values[:past], preferred_element_type=jnp.float32)
            mixed += jnp.dot(late.astype(jnp.bfloat16), values[past:], preferred_element_type=jnp.float32)
            result = (mixed / totals).astype(jnp.bfloat16)
            for head in range(batch):
                column = (part * batch + head) * HEAD_SIZE
                outbox[step, :, column:column + HEAD_SIZE] = result[head * sub_rows:(head + 1) * sub_rows]
        own = is_self(target_cp)

        @pl.when(jnp.logical_not(own))
        def _():
            remote(step, target_cp).start()

        @pl.when(own)
        def _():
            local(step).start()

        return carry

    lax.fori_loop(0, steps, one_step, 0)

    def finish(step, carry):
        target_cp = target_of(step // groups)
        own = is_self(target_cp)

        @pl.when(jnp.logical_not(own))
        def _():
            remote(step, target_cp).wait_send()

        @pl.when(own)
        def _():
            local(step).wait()

        return carry

    lax.fori_loop(0, steps, finish, 0)

    def arrive(slot, carry):
        group = lax.rem(slot, groups)
        from_tp = lax.rem(slot // groups, tp_count)
        from_sub = slot // (groups * tp_count)
        from_cp = tp_index * held + from_sub

        @pl.when(jnp.logical_not(jnp.logical_and(from_cp == cp_index, from_tp == tp_index)))
        def _():
            column = pl.multiple_of((from_tp * groups + group) * width, width)
            row = pl.multiple_of(from_sub * sub_rows, sub_rows)
            pltpu.make_async_remote_copy(
                src_ref=outbox.at[0],
                dst_ref=out_ref.at[pl.ds(row, sub_rows), pl.ds(column, width)],
                send_sem=send_sem.at[0],
                recv_sem=recv_sem.at[slot],
                device_id=(from_cp, from_tp),
                device_id_type=pl.DeviceIdType.MESH,
            ).wait_recv()

        return carry

    lax.fori_loop(0, held * tp_count * groups, arrive, 0)


def on_device(query_rows, token_keys, token_values, doc_lengths, block_plan):
    query_heads, key_heads, value_heads = (
        lax.all_to_all(query_rows, "tp", split_axis=1, concat_axis=0, tiled=True),
        lax.all_to_all(token_keys, "tp", split_axis=1, concat_axis=0, tiled=True),
        lax.all_to_all(token_values, "tp", split_axis=1, concat_axis=0, tiled=True),
    )
    block_rows = query_heads.shape[0]
    cp_count = lax.axis_size("cp")
    tp_count = lax.axis_size("tp")
    cp_index = lax.axis_index("cp")
    sequence = block_rows * cp_count
    sub_rows = block_rows // cp_count
    groups = key_heads.shape[1] // HEAD_SIZE
    per_group = query_heads.shape[1] // HEAD_SIZE // groups
    positions = cp_index * block_rows + jnp.arange(block_rows, dtype=jnp.int32)
    cosine_rows, sine_table = rotation_rows(positions, HEAD_SIZE, sequence)
    rotary_keys = apply_rotary_heads(
        key_heads.astype(jnp.float32).reshape(block_rows, groups, HEAD_SIZE), cosine_rows, sine_table
    ).astype(jnp.bfloat16)
    packed = jnp.concatenate([rotary_keys.reshape(block_rows, groups * HEAD_SIZE), value_heads], axis=1)
    reach_blocks = DOC_MOST // block_rows
    earlier = [shifted(packed, "cp", distance) for distance in range(reach_blocks, 0, -1)]
    window_rows = jnp.concatenate(earlier + [packed], axis=0)
    window_pos = (cp_index - reach_blocks) * block_rows + jnp.arange(
        (reach_blocks + 1) * block_rows, dtype=jnp.int32
    )
    doc_ends = jnp.cumsum(doc_lengths)
    lanes = jnp.arange(HEAD_SIZE, dtype=jnp.int32)[None, :]

    def document(pos):
        index = jnp.sum((doc_ends[None, :] <= pos[:, None]).astype(jnp.int32), axis=1)
        return jnp.where(pos < 0, HEAD_SIZE - 1, index)[:, None]

    key_marks = (document(window_pos) == lanes).astype(jnp.bfloat16)
    query_marks = jnp.where(document(positions) == lanes, 0.0, -1e30).astype(jnp.bfloat16)
    window_keys = jnp.stack(
        [
            jnp.concatenate([window_rows[:, g * HEAD_SIZE:(g + 1) * HEAD_SIZE], key_marks], axis=1)
            for g in range(groups)
        ]
    )
    window_values = jnp.stack(
        [window_rows[:, (groups + g) * HEAD_SIZE:(groups + g + 1) * HEAD_SIZE] for g in range(groups)]
    )
    scale = math.log2(math.e) / math.sqrt(HEAD_SIZE)
    cosine_wide = jnp.concatenate([cosine_rows, cosine_rows], axis=1) * scale
    sine_wide = jnp.concatenate([-sine_table, sine_table], axis=1) * scale
    window = DOC_MOST + sub_rows
    steps = cp_count * groups
    width = per_group * HEAD_SIZE
    vmem = pl.BlockSpec(memory_space=pltpu.VMEM)
    return pl.pallas_call(
        functools.partial(
            attend_and_place, cp_count, tp_count, (block_rows, sub_rows, groups, per_group, window)
        ),
        out_shape=jax.ShapeDtypeStruct(query_rows.shape, jnp.bfloat16),
        in_specs=[pl.BlockSpec(memory_space=pltpu.SMEM)] + [vmem] * 6,
        out_specs=pl.BlockSpec(memory_space=pl.ANY),
        scratch_shapes=[
            pltpu.VMEM((steps, sub_rows, width), jnp.bfloat16),
            pltpu.SemaphoreType.DMA((steps,)),
            pltpu.SemaphoreType.DMA((steps,)),
            pltpu.SemaphoreType.DMA((groups,)),
        ],
        compiler_params=pltpu.CompilerParams(has_side_effects=True, vmem_limit_bytes=60 * 2**20),
    )(
        block_plan,
        query_heads.reshape(cp_count, sub_rows, -1),
        cosine_wide.reshape(cp_count, sub_rows, -1),
        sine_wide.reshape(cp_count, sub_rows, -1),
        query_marks.reshape(cp_count, sub_rows, -1),
        window_keys.reshape(groups, -1, sub_rows, 2 * HEAD_SIZE),
        window_values.reshape(groups, -1, sub_rows, HEAD_SIZE),
    )


def solution(mesh):
    placed = (P(("cp", "tp"), None), P(("cp", "tp"), None), P(("cp", "tp"), None), P(), P())
    return jax.shard_map(
        on_device, mesh=mesh, in_specs=placed, out_specs=P(("cp", "tp"), None), check_vma=False
    )
```

time: 491 us -> 247 us (0.50); the launches traced: 486 us -> 247 us
  blocking collectives: 181 us -> 0 us
  Pallas kernels: 0 us -> 167 us
  matrix products: 141 us -> 1.54 us
  local copies, waits for them, and re-layouts: 85.5 us -> 16.5 us
  waiting for transfers between devices: 5.54 us -> 23.7 us
  starting transfers between devices: 46.6 us -> 28.8 us
  other arithmetic: 20.1 us -> 8.88 us
  loops' own time: 5.85 us -> 0 us
    all_to_all x2 -> x0, blocking collectives: 181 us -> none  [the longest x1 130 us: on_device(): lax.all_to_all(as_sent(outgoing), 'cp', split_axis=0, concat_axis=0, tile...]
    pallas_call x0 -> x1, Pallas kernels: none -> 167 us  [on_device(): pl.pallas_call(functools.partial(attend_and_place, cp_count, tp_count, (b...]
    sub x8 -> x0, matrix products: 92 us -> none  [attend(): raised = jnp.where(allowed, jnp.exp(masked - highest), 0.0)]
    dot_general x8 -> x0, matrix products: 47.7 us -> none  [attend(): jnp.einsum('ghrw,wgd->rghd', weights, value_window, preferred_element_typ...]
    dynamic_slice x32 -> x0, local copies, waits for them, and re-layouts: 30.4 us -> none  [the longest x8 23.8 us: attend_tile(): lax.dynamic_slice_in_dim(window_keys, offset, window_span, 0)]
    ppermute x8 -> x4, starting transfers between devices: 32.8 us -> 15.6 us  [shifted(): return lax.ppermute(x, axis, pairs)]
    ppermute x8 -> x4, waiting for transfers between devices: 1.54 us -> 18.7 us  [shifted(): return lax.ppermute(x, axis, pairs)]
    all_to_all x2 -> x0, local copies, waits for them, and re-layouts: 12.7 us -> none  [on_device(): lax.all_to_all(as_sent(placed), 'tp', split_axis=0, concat_axis=1, tiled=...]
  transfers between devices with their start and end apart: 11 -> 7, of which waited for: 2 -> 4; matrix products, arithmetic and copies ran while one was open for 4% -> 8% of each run, Pallas kernels for 0% -> 0%
where the time goes in v1:
time: 247 us
  Pallas kernels  167 us (68%)
  starting transfers between devices  28.8 us (12%)
  waiting for transfers between devices  23.7 us (10%)
  local copies, waits for them, and re-layouts  16.5 us (7%)
  other arithmetic  8.88 us (4%)
    pallas_call x1, Pallas kernels, on_device(): pl.pallas_call(functools.partial(attend_and_place, cp_count, tp_count, (b...  167 us
    ppermute x4, waiting for transfers between devices, shifted(): return lax.ppermute(x, axis, pairs)  18.7 us
    ppermute x4, starting transfers between devices, shifted(): return lax.ppermute(x, axis, pairs)  15.6 us
    unnamed x19, local copies, waits for them, and re-layouts  8.08 us
    all_to_all x1, starting transfers between devices, on_device(): lax.all_to_all(query_rows, 'tp', split_axis=1, concat_axis=0, tiled=True)  6.44 us
  transfers between devices with their start and end apart: 7, of which 4 were waited for; matrix products, arithmetic and copies ran while one was open for 8% of the time, Pallas kernels for 0%

profile of v1, /device:TPU:2, one launch (start us, length us, event | category | flops | bytes accessed | tf_op | source)
XLA Modules:
  0.0 246.7 jit_solution(1239941223396497516)
XLA Ops:
  0.0 1.7 copy.58
  1.7 3.4 %all-to-all-start.1 = ((bf16[128,4,256]{2,0,1:T(8,128)(2,1)}), bf16[128,4,256]{2,0,1:T(8,128)(2,1)S(1)}, u32[]{:S(2)}, u32[]{:S(2)}) async-start(bf16[128,4,256]{2,0,1:T(8,128)(2,1)} %bitcast.33), calls=%async_computation.1 | async-start | bytes 524288 | tf_op jit(solution)/shard_map/all_to_all | solution.py:221
  5.1 4.7 %copy.56 = bf16[16,4,8,4096]{3,2,0,1:T(8,128)(2,1)} copy(bf16[16,4,8,4096]{3,2,1,0:T(8,128)(2,1)} %bitcast.37) | data formatting | bytes 8388608 | tf_op jit(solution)/shard_map/all_to_all | solution.py:220
  12.1 1.2 fusion
  13.6 0.9 copy.49
  14.5 3.4 %all-to-all-start.2 = ((bf16[128,4,256]{2,0,1:T(8,128)(2,1)}), bf16[128,4,256]{2,0,1:T(8,128)(2,1)S(1)}, u32[]{:S(2)}, u32[]{:S(2)}) async-start(bf16[128,4,256]{2,0,1:T(8,128)(2,1)} %copy.49), calls=%async_computation.2 | async-start | bytes 524288 | tf_op jit(solution)/shard_map/all_to_all | solution.py:222
  18.2 3.9 %all-to-all-done.2 = bf16[128,4,256]{2,0,1:T(8,128)(2,1)S(1)} async-done(((bf16[128,4,256]{2,0,1:T(8,128)(2,1)}), bf16[128,4,256]{2,0,1:T(8,128)(2,1)S(1)}, u32[]{:S(2)}, u32[]{:S(2)}) %all-to-all-start.2) | async-done | bytes 262176 | tf_op jit(solution)/shard_map/all_to_all | solution.py:222
  22.2 6.4 %all-to-all-start = ((bf16[128,4,4096]{2,0,1:T(8,128)(2,1)}), bf16[128,4,4096]{2,0,1:T(8,128)(2,1)}, u32[]{:S(2)}, u32[]{:S(2)}) async-start(bf16[128,4,4096]{2,0,1:T(8,128)(2,1)} %bitcast.34), calls=%async_computation | async-start | bytes 8388608 | tf_op jit(solution)/shard_map/all_to_all | solution.py:220
  30.2 5.9 %collective-permute-start = (bf16[512,512]{1,0:T(8,128)(2,1)S(1)}, bf16[512,512]{1,0:T(8,128)(2,1)}, u32[]{:S(2)}, u32[]{:S(2)}) collective-permute-start(bf16[512,512]{1,0:T(8,128)(2,1)S(1)} %pad_maximum_fusion.4), channel_id=1, source_target_pairs={{0,16},{4,20},{8,24},{12,28},{1,17},{5,21},{9,25},{13,29},{2,18},{... | collective-permute-start | bytes 1572872 | tf_op jit(solution)/shard_map/ppermute | solution.py:19
  36.1 5.2 %collective-permute-start.1 = (bf16[512,512]{1,0:T(8,128)(2,1)S(1)}, bf16[512,512]{1,0:T(8,128)(2,1)}, u32[]{:S(2)}, u32[]{:S(2)}) collective-permute-start(bf16[512,512]{1,0:T(8,128)(2,1)S(1)} %pad_maximum_fusion.4), channel_id=1, source_target_pairs={{0,12},{4,16},{8,20},{12,24},{16,28},{1,13},{5,17},{9,21},{13,25},... | collective-permute-start | bytes 1572872 | tf_op jit(solution)/shard_map/ppermute | solution.py:19
  41.4 2.1 collective-permute-start.2
  44.3 2.3 collective-permute-start.3
  46.6 0.8 maximum_multiply_fusion.cosine_ref
  47.6 0.9 maximum_multiply_fusion.1.sine_ref
  48.5 1.1 constant_dynamic-update-slice_fusion.4
  49.5 9.4 %collective-permute-done.1 = bf16[512,512]{1,0:T(8,128)(2,1)} collective-permute-done((bf16[512,512]{1,0:T(8,128)(2,1)S(1)}, bf16[512,512]{1,0:T(8,128)(2,1)}, u32[]{:S(2)}, u32[]{:S(2)}) %collective-permute-start.1) | collective-permute-done | bytes 524320 | tf_op jit(solution)/shard_map/ppermute | solution.py:19
  58.9 1.1 constant_dynamic-update-slice_fusion.3
  60.0 9.3 %collective-permute-done.2 = bf16[512,512]{1,0:T(8,128)(2,1)} collective-permute-done((bf16[512,512]{1,0:T(8,128)(2,1)S(1)}, bf16[512,512]{1,0:T(8,128)(2,1)}, u32[]{:S(2)}, u32[]{:S(2)}) %collective-permute-start.2) | collective-permute-done | bytes 524320 | tf_op jit(solution)/shard_map/ppermute | solution.py:19
  69.3 1.1 constant_dynamic-update-slice_fusion.2
  71.0 1.2 pad_maximum_fusion.3.value_ref
  72.4 1.8 pad_maximum_fusion.key_ref
  74.2 1.0 all-to-all-done
  75.2 166.9 %shard_map.91 = bf16[128,16384]{1,0:T(8,128)(2,1)} custom-call(s32[8,8]{1,0:T(8,128)} %plan_ref.1, bf16[8,64,4096]{2,1,0:T(8,128)(2,1)} %bitcast.1.query_ref, f32[8,64,128]{2,1,0:T(8,128)} %maximum_multiply_fusion.cosine_ref, f32[8,64,128]{2,1,0:T(8,128)} %maximum_multiply_fusion.1.sine_ref, bf16[8,64,128]{2,1,0:T(8,128)(2,1)} %select_convert_fusion.mark_ref, ...), custom_call_target="tpu_custom_call" | custom-call | tf_op jit(solution)/shard_map/pallas_call | solution.py:269
  242.1 4.6 %copy.64 = bf16[128,16384]{1,0:T(8,128)(2,1)} copy(bf16[128,16384]{1,0:T(8,128)(2,1)} %shard_map.91) | data formatting | bytes 8388608
  (43 shorter events, 6.0 us)
Async XLA Ops:
  1.7 12.8 %all-to-all-start.1 = ((bf16[128,4,256]{2,0,1:T(8,128)(2,1)}), bf16[128,4,256]{2,0,1:T(8,128)(2,1)S(1)}, u32[]{:S(2)}, u32[]{:S(2)}) async-start(bf16[128,4,256]{2,0,1:T(8,128)(2,1)} %bitcast.33), calls=%async_computation.1 | async-start | bytes 524288 | tf_op jit(solution)/shard_map/all_to_all | solution.py:221
  5.1 4.8 %copy-start.2 = (f32[128,64]{1,0:T(8,128)S(1)}, f32[128,64]{1,0:T(8,128)}, u32[]{:S(2)}) copy-start(f32[128,64]{1,0:T(8,128)} %constant.65.clone) | copy-start | bytes 98308
  5.1 5.2 %copy-start.1 = (f32[128,64]{1,0:T(8,128)S(1)}, f32[128,64]{1,0:T(8,128)}, u32[]{:S(2)}) copy-start(f32[128,64]{1,0:T(8,128)} %constant.64.clone) | copy-start | bytes 98308
  5.1 5.6 %copy-start.4 = (f32[32,64]{1,0:T(8,128)S(1)}, f32[32,64]{1,0:T(8,128)}, u32[]{:S(2)}) copy-start(f32[32,64]{1,0:T(8,128)} %constant.63.clone) | copy-start | bytes 24580
  5.1 6.0 %copy-start.3 = (f32[32,64]{1,0:T(8,128)S(1)}, f32[32,64]{1,0:T(8,128)}, u32[]{:S(2)}) copy-start(f32[32,64]{1,0:T(8,128)} %constant.62.clone) | copy-start | bytes 24580
  5.1 6.6 %copy-start.5 = (s32[4]{0:T(128)S(1)}, s32[4]{0:T(128)}, u32[]{:S(2)}) copy-start(s32[4]{0:T(128)} %param.12) | copy-start | bytes 52
  9.9 3.6 %copy-start = (bf16[128,1024]{1,0:T(8,128)(2,1)S(1)}, bf16[128,1024]{1,0:T(8,128)(2,1)}, u32[]{:S(2)}) copy-start(bf16[128,1024]{1,0:T(8,128)(2,1)} %param.11) | copy-start | bytes 786436
  14.5 7.7 %all-to-all-start.2 = ((bf16[128,4,256]{2,0,1:T(8,128)(2,1)}), bf16[128,4,256]{2,0,1:T(8,128)(2,1)S(1)}, u32[]{:S(2)}, u32[]{:S(2)}) async-start(bf16[128,4,256]{2,0,1:T(8,128)(2,1)} %copy.49), calls=%async_computation.2 | async-start | bytes 524288 | tf_op jit(solution)/shard_map/all_to_all | solution.py:222
  22.2 53.0 %all-to-all-start = ((bf16[128,4,4096]{2,0,1:T(8,128)(2,1)}), bf16[128,4,4096]{2,0,1:T(8,128)(2,1)}, u32[]{:S(2)}, u32[]{:S(2)}) async-start(bf16[128,4,4096]{2,0,1:T(8,128)(2,1)} %bitcast.34), calls=%async_computation | async-start | bytes 8388608 | tf_op jit(solution)/shard_map/all_to_all | solution.py:220
  30.2 18.3 %collective-permute-start = (bf16[512,512]{1,0:T(8,128)(2,1)S(1)}, bf16[512,512]{1,0:T(8,128)(2,1)}, u32[]{:S(2)}, u32[]{:S(2)}) collective-permute-start(bf16[512,512]{1,0:T(8,128)(2,1)S(1)} %pad_maximum_fusion.4), channel_id=1, source_target_pairs={{0,16},{4,20},{8,24},{12,28},{1,17},{5,21},{9,25},{13,29},{2,18},{... | collective-permute-start | bytes 1572872 | tf_op jit(solution)/shard_map/ppermute | solution.py:19
  36.1 22.8 %collective-permute-start.1 = (bf16[512,512]{1,0:T(8,128)(2,1)S(1)}, bf16[512,512]{1,0:T(8,128)(2,1)}, u32[]{:S(2)}, u32[]{:S(2)}) collective-permute-start(bf16[512,512]{1,0:T(8,128)(2,1)S(1)} %pad_maximum_fusion.4), channel_id=1, source_target_pairs={{0,12},{4,16},{8,20},{12,24},{16,28},{1,13},{5,17},{9,21},{13,25},... | collective-permute-start | bytes 1572872 | tf_op jit(solution)/shard_map/ppermute | solution.py:19
  41.4 28.0 %collective-permute-start.2 = (bf16[512,512]{1,0:T(8,128)(2,1)S(1)}, bf16[512,512]{1,0:T(8,128)(2,1)}, u32[]{:S(2)}, u32[]{:S(2)}) collective-permute-start(bf16[512,512]{1,0:T(8,128)(2,1)S(1)} %pad_maximum_fusion.4), channel_id=1, source_target_pairs={{0,8},{4,12},{8,16},{12,20},{16,24},{20,28},{1,9},{5,13},{9,17},{1... | collective-permute-start | bytes 1572872 | tf_op jit(solution)/shard_map/ppermute | solution.py:19
  44.3 26.1 %collective-permute-start.3 = (bf16[512,512]{1,0:T(8,128)(2,1)S(1)}, bf16[512,512]{1,0:T(8,128)(2,1)S(1)}, u32[]{:S(2)}, u32[]{:S(2)}) collective-permute-start(bf16[512,512]{1,0:T(8,128)(2,1)S(1)} %pad_maximum_fusion.4), channel_id=1, source_target_pairs={{0,4},{4,8},{8,12},{12,16},{16,20},{20,24},{24,28},{1,5},{5,9},{9,... | collective-permute-start | bytes 1572872 | tf_op jit(solution)/shard_map/ppermute | solution.py:19

commit v2 on v1

--- a/solution.py
+++ b/solution.py
@@ -88,11 +88,20 @@
     past = window - sub_rows
 
     def target_of(order):
-        if cp_count % 2:
+        if cp_count % 4:
             return lax.rem(cp_index + order, cp_count)
         half = cp_count // 2
-        side = lax.rem(cp_index // half + 1 + order // half, 2)
-        return side * half + lax.rem(cp_index + order, half)
+        quarter = cp_count // 4
+        mine = cp_index // quarter
+        outer = 1 - ((mine + 1) // 2) % 2
+        near_first = jnp.where(
+            order < quarter, order + half, jnp.where(order < half + quarter, order - quarter, order)
+        )
+        place = jnp.where(outer == 1, near_first, order)
+        across = (1 - cp_index // half) * half + (cp_index + place) % half
+        beside = (mine // 2 * 2 + 1 - mine % 2) * quarter + (cp_index + place) % quarter
+        within = mine * quarter + (cp_index + 1 + place) % quarter
+        return jnp.where(place < half, across, jnp.where(place < half + quarter, beside, within))
 
     def remote(step, target_cp):
         group = lax.rem(step, groups)
@@ -216,14 +225,17 @@
 
 
 def on_device(query_rows, token_keys, token_values, doc_lengths, block_plan):
-    query_heads, key_heads, value_heads = (
-        lax.all_to_all(query_rows, "tp", split_axis=1, concat_axis=0, tiled=True),
-        lax.all_to_all(token_keys, "tp", split_axis=1, concat_axis=0, tiled=True),
-        lax.all_to_all(token_values, "tp", split_axis=1, concat_axis=0, tiled=True),
-    )
+    tp_count = lax.axis_size("tp")
+    own_rows = token_keys.shape[0]
+    paired = jnp.concatenate(
+        [token_keys.reshape(own_rows, tp_count, -1), token_values.reshape(own_rows, tp_count, -1)], axis=2
+    ).reshape(own_rows, -1)
+    paired_heads = lax.all_to_all(paired, "tp", split_axis=1, concat_axis=0, tiled=True)
+    query_heads = lax.all_to_all(query_rows, "tp", split_axis=1, concat_axis=0, tiled=True)
+    key_heads = paired_heads[:, : paired_heads.shape[1] // 2]
+    value_heads = paired_heads[:, paired_heads.shape[1] // 2 :]
     block_rows = query_heads.shape[0]
     cp_count = lax.axis_size("cp")
-    tp_count = lax.axis_size("tp")
     cp_index = lax.axis_index("cp")
     sequence = block_rows * cp_count
     sub_rows = block_rows // cp_count
@@ -236,8 +248,11 @@
     ).astype(jnp.bfloat16)
     packed = jnp.concatenate([rotary_keys.reshape(block_rows, groups * HEAD_SIZE), value_heads], axis=1)
     reach_blocks = DOC_MOST // block_rows
-    earlier = [shifted(packed, "cp", distance) for distance in range(reach_blocks, 0, -1)]
-    window_rows = jnp.concatenate(earlier + [packed], axis=0)
+    blocks = [packed]
+    for distance in range(1, reach_blocks + 1):
+        step = min(2, distance)
+        blocks.append(shifted(blocks[distance - step], "cp", step))
+    window_rows = jnp.concatenate(blocks[::-1], axis=0)
     window_pos = (cp_index - reach_blocks) * block_rows + jnp.arange(
         (reach_blocks + 1) * block_rows, dtype=jnp.int32
     )

time: 247 us -> 210 us (0.85)
  Pallas kernels: 167 us -> 136 us
  waiting for transfers between devices: 23.7 us -> 12.7 us
  starting transfers between devices: 28.8 us -> 35 us
    pallas_call x1, Pallas kernels: 167 us -> 136 us  [on_device(): pl.pallas_call(functools.partial(attend_and_place, cp_count, tp_count, (b...]
    ppermute x4, starting transfers between devices: 15.6 us -> 25.1 us  [shifted(): return lax.ppermute(x, axis, pairs)]
    ppermute x4, waiting for transfers between devices: 18.7 us -> 12.6 us  [shifted(): return lax.ppermute(x, axis, pairs)]
    all_to_all x2 -> x1, waiting for transfers between devices: 3.94 us -> 0.1 us  [on_device(): lax.all_to_all(paired, 'tp', split_axis=1, concat_axis=0, tiled=True)]
    all_to_all x2 -> x1, starting transfers between devices: 6.79 us -> 3.46 us  [on_device(): lax.all_to_all(paired, 'tp', split_axis=1, concat_axis=0, tiled=True)]
    all_to_all x2 -> x0, local copies, waits for them, and re-layouts: 2.54 us -> none  [the longest x1 1.68 us: on_device(): lax.all_to_all(token_keys, 'tp', split_axis=1, concat_axis=0, tiled=True)]
    unnamed x19 -> x18, local copies, waits for them, and re-layouts: 8.08 us -> 8.09 us
  transfers between devices with their start and end apart: 7 -> 6, of which waited for: 4 -> 3; matrix products, arithmetic and copies ran while one was open for 8% -> 8% of each run, Pallas kernels for 0% -> 0%
where the time goes in v2:
time: 210 us; the launch traced here: 209 us
  Pallas kernels  136 us (65%)
  starting transfers between devices  35 us (17%)
  local copies, waits for them, and re-layouts  15 us (7%)
  waiting for transfers between devices  12.7 us (6%)
  other arithmetic  8.93 us (4%)
    pallas_call x1, Pallas kernels, on_device(): pl.pallas_call(functools.partial(attend_and_place, cp_count, tp_count, (b...  136 us
    ppermute x4, starting transfers between devices, shifted(): return lax.ppermute(x, axis, pairs)  25.1 us
    ppermute x4, waiting for transfers between devices, shifted(): return lax.ppermute(x, axis, pairs)  12.6 us
    unnamed x18, local copies, waits for them, and re-layouts  8.09 us
    all_to_all x1, starting transfers between devices, on_device(): lax.all_to_all(query_rows, 'tp', split_axis=1, concat_axis=0, tiled=True)  6.44 us
    all_to_all x1, local copies, waits for them, and re-layouts, on_device(): lax.all_to_all(query_rows, 'tp', split_axis=1, concat_axis=0, tiled=True)  4.7 us
  transfers between devices with their start and end apart: 6, of which 3 were waited for; matrix products, arithmetic and copies ran while one was open for 8% of the time, Pallas kernels for 0%

profile of v2, /device:TPU:2, one launch (start us, length us, event | category | flops | bytes accessed | tf_op | source)
XLA Modules:
  0.0 209.3 jit_solution(4540250582256480931)
XLA Ops:
  0.0 1.2 copy.37
  1.2 1.1 copy.36
  2.4 1.0 copy.38
  3.4 3.5 %all-to-all-start.1 = ((bf16[128,4,512]{2,0,1:T(8,128)(2,1)}), bf16[128,4,512]{2,0,1:T(8,128)(2,1)S(1)}, u32[]{:S(2)}, u32[]{:S(2)}) async-start(bf16[128,4,512]{2,0,1:T(8,128)(2,1)} %copy.38), calls=%async_computation.1 | async-start | bytes 1048576 | tf_op jit(solution)/shard_map/all_to_all | solution.py:233
  8.5 4.7 %copy.45 = bf16[16,4,8,4096]{3,2,0,1:T(8,128)(2,1)} copy(bf16[16,4,8,4096]{3,2,1,0:T(8,128)(2,1)} %bitcast.32) | data formatting | bytes 8388608 | tf_op jit(solution)/shard_map/all_to_all | solution.py:234
  13.8 6.4 %all-to-all-start = ((bf16[128,4,4096]{2,0,1:T(8,128)(2,1)}), bf16[128,4,4096]{2,0,1:T(8,128)(2,1)}, u32[]{:S(2)}, u32[]{:S(2)}) async-start(bf16[128,4,4096]{2,0,1:T(8,128)(2,1)} %bitcast.29), calls=%async_computation | async-start | bytes 8388608 | tf_op jit(solution)/shard_map/all_to_all | solution.py:234
  20.6 0.8 subtract_convert_fusion
  21.4 0.7 pad_maximum_fusion.6
  22.2 4.2 %collective-permute-start = (bf16[512,512]{1,0:T(8,128)(2,1)S(1)}, bf16[512,512]{1,0:T(8,128)(2,1)S(1)}, u32[]{:S(2)}, u32[]{:S(2)}) collective-permute-start(bf16[512,512]{1,0:T(8,128)(2,1)S(1)} %pad_maximum_fusion.5), channel_id=1, source_target_pairs={{0,8},{4,12},{8,16},{12,20},{16,24},{20,28},{1,9},{5,13},{9,17},{1... | collective-permute-start | bytes 1572872 | tf_op jit(solution)/shard_map/ppermute | solution.py:19
  26.4 3.5 %collective-permute-start.2 = (bf16[512,512]{1,0:T(8,128)(2,1)S(1)}, bf16[512,512]{1,0:T(8,128)(2,1)S(1)}, u32[]{:S(2)}, u32[]{:S(2)}) collective-permute-start(bf16[512,512]{1,0:T(8,128)(2,1)S(1)} %pad_maximum_fusion.5), channel_id=1, source_target_pairs={{0,4},{4,8},{8,12},{12,16},{16,20},{20,24},{24,28},{1,5},{5,9},{9,... | collective-permute-start | bytes 1572872 | tf_op jit(solution)/shard_map/ppermute | solution.py:19
  29.9 1.2 fusion
  31.3 6.6 %collective-permute-done = bf16[512,512]{1,0:T(8,128)(2,1)S(1)} collective-permute-done((bf16[512,512]{1,0:T(8,128)(2,1)S(1)}, bf16[512,512]{1,0:T(8,128)(2,1)S(1)}, u32[]{:S(2)}, u32[]{:S(2)}) %collective-permute-start) | collective-permute-done | bytes 524320 | tf_op jit(solution)/shard_map/ppermute | solution.py:19
  37.8 5.2 %collective-permute-start.1 = (bf16[512,512]{1,0:T(8,128)(2,1)S(1)}, bf16[512,512]{1,0:T(8,128)(2,1)}, u32[]{:S(2)}, u32[]{:S(2)}) collective-permute-start(bf16[512,512]{1,0:T(8,128)(2,1)S(1)} %collective-permute-done), channel_id=1, source_target_pairs={{0,8},{4,12},{8,16},{12,20},{16,24},{20,28},{1,9},{5,13},{9,17},{1... | collective-permute-start | bytes 1572872 | tf_op jit(solution)/shard_map/ppermute | solution.py:19
  43.0 12.2 %collective-permute-start.3 = (bf16[512,512]{1,0:T(8,128)(2,1)S(1)}, bf16[512,512]{1,0:T(8,128)(2,1)S(1)}, u32[]{:S(2)}, u32[]{:S(2)}) collective-permute-start(bf16[512,512]{1,0:T(8,128)(2,1)S(1)} %collective-permute-done.2), channel_id=1, source_target_pairs={{0,8},{4,12},{8,16},{12,20},{16,24},{20,28},{1,9},{5,13},{9,17},{1... | collective-permute-start | bytes 1572872 | tf_op jit(solution)/shard_map/ppermute | solution.py:19
  55.3 0.9 maximum_multiply_fusion.cosine_ref
  56.3 0.8 maximum_multiply_fusion.1.sine_ref
  57.1 0.8 select_convert_fusion.mark_ref
  57.9 1.1 constant_dynamic-update-slice_fusion.4
  59.0 6.0 %collective-permute-done.3 = bf16[512,512]{1,0:T(8,128)(2,1)S(1)} collective-permute-done((bf16[512,512]{1,0:T(8,128)(2,1)S(1)}, bf16[512,512]{1,0:T(8,128)(2,1)S(1)}, u32[]{:S(2)}, u32[]{:S(2)}) %collective-permute-start.3) | collective-permute-done | bytes 524320 | tf_op jit(solution)/shard_map/ppermute | solution.py:19
  65.2 0.5 fusion.14
  65.6 1.2 pad_maximum_fusion.3.value_ref
  67.0 1.8 pad_maximum_fusion.key_ref
  68.8 135.9 %shard_map.91 = bf16[128,16384]{1,0:T(8,128)(2,1)} custom-call(s32[8,8]{1,0:T(8,128)} %plan_ref.1, bf16[8,64,4096]{2,1,0:T(8,128)(2,1)} %bitcast.1.query_ref, f32[8,64,128]{2,1,0:T(8,128)} %maximum_multiply_fusion.cosine_ref, f32[8,64,128]{2,1,0:T(8,128)} %maximum_multiply_fusion.1.sine_ref, bf16[8,64,128]{2,1,0:T(8,128)(2,1)} %select_convert_fusion.mark_ref, ...), custom_call_target="tpu_custom_call" | custom-call | tf_op jit(solution)/shard_map/pallas_call | solution.py:284
  204.8 4.6 %copy.52 = bf16[128,16384]{1,0:T(8,128)(2,1)} copy(bf16[128,16384]{1,0:T(8,128)(2,1)} %shard_map.91) | data formatting | bytes 8388608
  (40 shorter events, 3.3 us)
Async XLA Ops:
  0.0 6.9 %copy-start.1 = (f32[128,64]{1,0:T(8,128)S(1)}, f32[128,64]{1,0:T(8,128)}, u32[]{:S(2)}) copy-start(f32[128,64]{1,0:T(8,128)} %constant.65.clone) | copy-start | bytes 98308
  0.0 7.2 %copy-start = (f32[128,64]{1,0:T(8,128)S(1)}, f32[128,64]{1,0:T(8,128)}, u32[]{:S(2)}) copy-start(f32[128,64]{1,0:T(8,128)} %constant.64.clone) | copy-start | bytes 98308
  0.0 7.6 %copy-start.3 = (f32[32,64]{1,0:T(8,128)S(1)}, f32[32,64]{1,0:T(8,128)}, u32[]{:S(2)}) copy-start(f32[32,64]{1,0:T(8,128)} %constant.63.clone) | copy-start | bytes 24580
  0.0 8.0 %copy-start.2 = (f32[32,64]{1,0:T(8,128)S(1)}, f32[32,64]{1,0:T(8,128)}, u32[]{:S(2)}) copy-start(f32[32,64]{1,0:T(8,128)} %constant.62.clone) | copy-start | bytes 24580
  3.4 10.5 %all-to-all-start.1 = ((bf16[128,4,512]{2,0,1:T(8,128)(2,1)}), bf16[128,4,512]{2,0,1:T(8,128)(2,1)S(1)}, u32[]{:S(2)}, u32[]{:S(2)}) async-start(bf16[128,4,512]{2,0,1:T(8,128)(2,1)} %copy.38), calls=%async_computation.1 | async-start | bytes 1048576 | tf_op jit(solution)/shard_map/all_to_all | solution.py:233
  8.4 5.0 %copy-start.4 = (s32[4]{0:T(128)S(1)}, s32[4]{0:T(128)}, u32[]{:S(2)}) copy-start(s32[4]{0:T(128)} %param.12) | copy-start | bytes 52
  13.8 55.0 %all-to-all-start = ((bf16[128,4,4096]{2,0,1:T(8,128)(2,1)}), bf16[128,4,4096]{2,0,1:T(8,128)(2,1)}, u32[]{:S(2)}, u32[]{:S(2)}) async-start(bf16[128,4,4096]{2,0,1:T(8,128)(2,1)} %bitcast.29), calls=%async_computation | async-start | bytes 8388608 | tf_op jit(solution)/shard_map/all_to_all | solution.py:234
  22.2 15.6 %collective-permute-start = (bf16[512,512]{1,0:T(8,128)(2,1)S(1)}, bf16[512,512]{1,0:T(8,128)(2,1)S(1)}, u32[]{:S(2)}, u32[]{:S(2)}) collective-permute-start(bf16[512,512]{1,0:T(8,128)(2,1)S(1)} %pad_maximum_fusion.5), channel_id=1, source_target_pairs={{0,8},{4,12},{8,16},{12,20},{16,24},{20,28},{1,9},{5,13},{9,17},{1... | collective-permute-start | bytes 1572872 | tf_op jit(solution)/shard_map/ppermute | solution.py:19
  26.4 16.6 %collective-permute-start.2 = (bf16[512,512]{1,0:T(8,128)(2,1)S(1)}, bf16[512,512]{1,0:T(8,128)(2,1)S(1)}, u32[]{:S(2)}, u32[]{:S(2)}) collective-permute-start(bf16[512,512]{1,0:T(8,128)(2,1)S(1)} %pad_maximum_fusion.5), channel_id=1, source_target_pairs={{0,4},{4,8},{8,12},{12,16},{16,20},{20,24},{24,28},{1,5},{5,9},{9,... | collective-permute-start | bytes 1572872 | tf_op jit(solution)/shard_map/ppermute | solution.py:19
  37.8 20.1 %collective-permute-start.1 = (bf16[512,512]{1,0:T(8,128)(2,1)S(1)}, bf16[512,512]{1,0:T(8,128)(2,1)}, u32[]{:S(2)}, u32[]{:S(2)}) collective-permute-start(bf16[512,512]{1,0:T(8,128)(2,1)S(1)} %collective-permute-done), channel_id=1, source_target_pairs={{0,8},{4,12},{8,16},{12,20},{16,24},{20,28},{1,9},{5,13},{9,17},{1... | collective-permute-start | bytes 1572872 | tf_op jit(solution)/shard_map/ppermute | solution.py:19
  43.0 22.0 %collective-permute-start.3 = (bf16[512,512]{1,0:T(8,128)(2,1)S(1)}, bf16[512,512]{1,0:T(8,128)(2,1)S(1)}, u32[]{:S(2)}, u32[]{:S(2)}) collective-permute-start(bf16[512,512]{1,0:T(8,128)(2,1)S(1)} %collective-permute-done.2), channel_id=1, source_target_pairs={{0,8},{4,12},{8,16},{12,20},{16,24},{20,28},{1,9},{5,13},{9,17},{1... | collective-permute-start | bytes 1572872 | tf_op jit(solution)/shard_map/ppermute | solution.py:19
